TPU v7x, 32 devices: a whole 2x2x4 slice. The times are simulated.
32 devices in a mesh: gx: 4 (over x, core), gy: 4 (over z), gz: 2 (over y).
Axes of the slice: x: 2, y: 2, z: 4, core: 2. Of those that a mesh axis runs over, the one named last changes fastest.
Arguments:
- columns: int32 [1024, 2048], P(('gx', 'gy', 'gz')), may hold values from 0 to 32767, as said below
- counts: int32 [1024, 2048], P(('gx', 'gy', 'gz')), may hold values from 1 to 63
- nnz_count: int32 [1024], P(('gx', 'gy', 'gz')), may hold values from 1 to 2048, as said below
- selected: int32 [2048], replicated, may hold values from 0 to 32767, as said below
Outputs:
- gene_stats: float32 [2, 32768], P(None, 'gz')
- pca_input: bfloat16 [1024, 2048], P(('gx', 'gy'), 'gz')
Inputs may be any that keep to these rules, and one draw needn't show every extreme that they name: `columns`: in each row no two slots fall in the same block of 16 consecutive genes (so the first nnz_count slots hold distinct genes); slots beyond nnz_count are not part of the matrix. For every k, the live slots of one cell fall on at most 128 of the genes selected[k * 2048 / 2] to selected[(k + 1) * 2048 / 2 - 1]; some cell reaches 128 for every k in every draw. `nnz_count`: some cell has all 2048 slots live in every draw. `selected`: distinct genes.
All inputs are finite; a program needn't handle non-finite values.
Results may differ from a plain program's by a relative error of at most 0.0085.
Values may be sent and summed in bfloat16 or wider, within the bound.
No kernel may reach another device: no remote copies, remote signals or barrier semaphores. Data moves between devices by JAX's collectives and lax.ppermute only.
A program may use at most 128 MiB of HBM per device.

v0:
```python
import jax
import jax.numpy as jnp
from jax import lax
from jax.sharding import PartitionSpec as P

GENES = 32768
SEL = 2048
target_sum = 10000.0
var_floor = 0.01
clip_value = 10.0
lane_count = 256


def standardize(dense, mean_sel, variance_sel):
    scale_sel = jnp.sqrt(jnp.maximum(variance_sel, var_floor))
    return jnp.clip((dense - mean_sel[None, :]) / scale_sel[None, :], -clip_value, clip_value)


def cell_block(pair):
    block_genes, block_values = pair
    high_count = GENES // lane_count
    high_ids = lax.broadcasted_iota(jnp.int32, (1, 1, high_count), 2)
    low_ids = lax.broadcasted_iota(jnp.int32, (1, 1, lane_count), 2)
    high_table = ((block_genes // lane_count)[:, :, None] == high_ids).astype(jnp.bfloat16)
    low_hit = (block_genes % lane_count)[:, :, None] == low_ids
    upper = lax.optimization_barrier(block_values.astype(jnp.bfloat16))
    lower = (block_values - upper.astype(jnp.float32)).astype(jnp.bfloat16)
    upper_table = jnp.where(low_hit, upper[:, :, None], jnp.bfloat16(0.0))
    lower_table = jnp.where(low_hit, lower[:, :, None], jnp.bfloat16(0.0))
    upper_part = jnp.einsum(
        "csh,csl->chl", high_table, upper_table, preferred_element_type=jnp.float32
    )
    lower_part = jnp.einsum(
        "csh,csl->chl", high_table, lower_table, preferred_element_type=jnp.float32
    )
    return upper_part + lower_part


def per_device(columns, counts, nnz_count, selected):
    local_cells = columns.shape[0]
    row_slots = columns.shape[1]
    owners = lax.axis_size("gz")
    owner_index = lax.axis_index("gz")
    cells = local_cells * lax.axis_size("gx") * lax.axis_size("gy") * owners
    slot = lax.broadcasted_iota(jnp.int32, counts.shape, 1)
    live = slot < nnz_count[:, None]
    raw = jnp.where(live, counts.astype(jnp.float32), jnp.float32(0.0))
    library = jnp.sum(raw, axis=1, keepdims=True)
    values = jnp.log1p(raw * (target_sum / library))
    genes = jnp.where(live, columns, 0)
    block_rows = 4
    block_total = local_cells // block_rows
    expanded = lax.map(
        cell_block,
        (
            genes.reshape(block_total, block_rows, row_slots),
            values.reshape(block_total, block_rows, row_slots),
        ),
    )
    expanded = expanded.reshape(local_cells, GENES)
    total = jnp.sum(expanded, axis=0)
    square = jnp.sum(expanded * expanded, axis=0)
    terms = jnp.stack([total, square])
    owned = GENES // owners
    sums = lax.psum(terms, ("gx", "gy", "gz"))
    own_sums = lax.dynamic_slice_in_dim(sums, owner_index * owned, owned, 1)
    picked_sums = jnp.take(sums, selected, axis=1)
    own_mean = own_sums[0] / cells
    own_variance = own_sums[1] / cells - own_mean * own_mean
    gene_stats = jnp.stack([own_mean, own_variance])
    sel_mean = picked_sums[0] / cells
    sel_variance = picked_sums[1] / cells - sel_mean * sel_mean
    dense = jnp.take(expanded, selected, axis=1)
    share_size = SEL // owners
    own_mean_sel = lax.dynamic_slice_in_dim(sel_mean, owner_index * share_size, share_size, 0)
    own_variance_sel = lax.dynamic_slice_in_dim(
        sel_variance, owner_index * share_size, share_size, 0
    )
    moved = lax.all_to_all(
        dense.astype(jnp.bfloat16), "gz", split_axis=1, concat_axis=0, tiled=True
    ).astype(dense.dtype)
    pca_input = standardize(moved, own_mean_sel, own_variance_sel).astype(jnp.bfloat16)
    return (gene_stats, pca_input)


def solution(mesh):
    return jax.shard_map(
        per_device,
        mesh=mesh,
        in_specs=(
            P(("gx", "gy", "gz"), None),
            P(("gx", "gy", "gz"), None),
            P(("gx", "gy", "gz")),
            P(),
        ),
        out_specs=(P(None, "gz"), P(("gx", "gy"), "gz")),
        check_vma=False,
    )
```

profile of v0, /device:TPU:0, one launch (start us, length us, event | category | flops | bytes accessed | tf_op | source)
XLA Modules:
  0.0 230.8 jit_solution(16225255947262282294)
XLA Ops:
  7.2 0.0 all-reduce.2.cloned.1.call-start
  7.2 1.2 fusion.36
  8.4 1.1 multiply_log-plus-one_fusion
  9.5 0.1 reshape.103
  9.6 1.0 fusion.35
  10.7 0.1 reshape.102
  10.8 56.9 %while.12 = (s32[]{:T(128)}, f32[8,4,128,256]{3,2,1,0:T(8,128)}, s32[8,4,2048]{2,1,0:T(4,128)S(1)}, f32[8,4,2048]{2,1,0:T(4,128)S(1)}, s32[]{:T(128)}) while((s32[]{:T(128)}, f32[8,4,128,256]{3,2,1,0:T(8,128)}, s32[8,4,2048]{2,1,0:T(4,128)S(1)}, f32[8,4,2048]{2,1,0:T(4,128)S(1)}, s32[]{:T(128)}) %tuple.39), condition=%wide.region_2.3_spmd, body=%wide.region_1.2_spmd.sunk | while | flops 1084588032 | bytes 1982553 | solution.py:53
  10.8 0.1 add_select_fusion.4
  10.9 3.2 %fusion.48 = f32[4,128,256]{2,1,0:T(8,128)S(1)} fusion(s32[4,2048]{1,0:T(4,128)S(1)} %add_select_fusion.5, bf16[4,2048]{1,0:T(4,128)(2,1)S(1)} %bitcast_convert_fusion.2, s32[4,2048]{1,0:T(4,128)S(1)} %get-tuple-element.109), kind=kOutput, calls=%fused_computation.5.clone.1 | convolution fusion | flops 542113792 | bytes 606208 | tf_op jit(solution)/shard_map/while/body/eval_jaxpr/csh,csl->chl/dot_general | solution.py:30
  14.1 3.8 %fusion.50 = f32[8,4,128,256]{3,2,1,0:T(8,128)} fusion(f32[8,4,128,256]{3,2,1,0:T(8,128)} %get-tuple-element.116, s32[]{:T(128)S(6)} %copy.30, f32[4,128,256]{2,1,0:T(8,128)S(1)} %fusion.48, s32[4,2048]{1,0:T(4,128)S(1)} %add_select_fusion.5, bf16[4,2048]{1,0:T(4,128)(2,1)S(1)} %fusion.49, s32[4,2048]{1,0:T(4,128)S(1)} %get-tuple-element.109), kind=kOutput, calls=%fused_computation.18.clone.1 | convolution fusion | flops 542244864 | bytes 1130500 | tf_op jit(solution)/shard_map/while/body/eval_jaxpr/csh,csl->chl/dot_general | solution.py:33
  17.9 0.1 add_select_fusion.4
  18.0 3.2 %fusion.48 = f32[4,128,256]{2,1,0:T(8,128)S(1)} fusion(s32[4,2048]{1,0:T(4,128)S(1)} %add_select_fusion.5, bf16[4,2048]{1,0:T(4,128)(2,1)S(1)} %bitcast_convert_fusion.2, s32[4,2048]{1,0:T(4,128)S(1)} %get-tuple-element.109), kind=kOutput, calls=%fused_computation.5.clone.1 | convolution fusion | flops 542113792 | bytes 606208 | tf_op jit(solution)/shard_map/while/body/eval_jaxpr/csh,csl->chl/dot_general | solution.py:30
  21.2 3.8 %fusion.50 = f32[8,4,128,256]{3,2,1,0:T(8,128)} fusion(f32[8,4,128,256]{3,2,1,0:T(8,128)} %get-tuple-element.116, s32[]{:T(128)S(6)} %copy.30, f32[4,128,256]{2,1,0:T(8,128)S(1)} %fusion.48, s32[4,2048]{1,0:T(4,128)S(1)} %add_select_fusion.5, bf16[4,2048]{1,0:T(4,128)(2,1)S(1)} %fusion.49, s32[4,2048]{1,0:T(4,128)S(1)} %get-tuple-element.109), kind=kOutput, calls=%fused_computation.18.clone.1 | convolution fusion | flops 542244864 | bytes 1130500 | tf_op jit(solution)/shard_map/while/body/eval_jaxpr/csh,csl->chl/dot_general | solution.py:33
  25.0 0.1 add_select_fusion.4
  25.1 3.2 %fusion.48 = f32[4,128,256]{2,1,0:T(8,128)S(1)} fusion(s32[4,2048]{1,0:T(4,128)S(1)} %add_select_fusion.5, bf16[4,2048]{1,0:T(4,128)(2,1)S(1)} %bitcast_convert_fusion.2, s32[4,2048]{1,0:T(4,128)S(1)} %get-tuple-element.109), kind=kOutput, calls=%fused_computation.5.clone.1 | convolution fusion | flops 542113792 | bytes 606208 | tf_op jit(solution)/shard_map/while/body/eval_jaxpr/csh,csl->chl/dot_general | solution.py:30
  28.3 3.8 %fusion.50 = f32[8,4,128,256]{3,2,1,0:T(8,128)} fusion(f32[8,4,128,256]{3,2,1,0:T(8,128)} %get-tuple-element.116, s32[]{:T(128)S(6)} %copy.30, f32[4,128,256]{2,1,0:T(8,128)S(1)} %fusion.48, s32[4,2048]{1,0:T(4,128)S(1)} %add_select_fusion.5, bf16[4,2048]{1,0:T(4,128)(2,1)S(1)} %fusion.49, s32[4,2048]{1,0:T(4,128)S(1)} %get-tuple-element.109), kind=kOutput, calls=%fused_computation.18.clone.1 | convolution fusion | flops 542244864 | bytes 1130500 | tf_op jit(solution)/shard_map/while/body/eval_jaxpr/csh,csl->chl/dot_general | solution.py:33
  32.1 0.1 add_select_fusion.4
  32.3 3.2 %fusion.48 = f32[4,128,256]{2,1,0:T(8,128)S(1)} fusion(s32[4,2048]{1,0:T(4,128)S(1)} %add_select_fusion.5, bf16[4,2048]{1,0:T(4,128)(2,1)S(1)} %bitcast_convert_fusion.2, s32[4,2048]{1,0:T(4,128)S(1)} %get-tuple-element.109), kind=kOutput, calls=%fused_computation.5.clone.1 | convolution fusion | flops 542113792 | bytes 606208 | tf_op jit(solution)/shard_map/while/body/eval_jaxpr/csh,csl->chl/dot_general | solution.py:30
  35.4 3.8 %fusion.50 = f32[8,4,128,256]{3,2,1,0:T(8,128)} fusion(f32[8,4,128,256]{3,2,1,0:T(8,128)} %get-tuple-element.116, s32[]{:T(128)S(6)} %copy.30, f32[4,128,256]{2,1,0:T(8,128)S(1)} %fusion.48, s32[4,2048]{1,0:T(4,128)S(1)} %add_select_fusion.5, bf16[4,2048]{1,0:T(4,128)(2,1)S(1)} %fusion.49, s32[4,2048]{1,0:T(4,128)S(1)} %get-tuple-element.109), kind=kOutput, calls=%fused_computation.18.clone.1 | convolution fusion | flops 542244864 | bytes 1130500 | tf_op jit(solution)/shard_map/while/body/eval_jaxpr/csh,csl->chl/dot_general | solution.py:33
  39.3 0.1 add_select_fusion.4
  39.4 3.2 %fusion.48 = f32[4,128,256]{2,1,0:T(8,128)S(1)} fusion(s32[4,2048]{1,0:T(4,128)S(1)} %add_select_fusion.5, bf16[4,2048]{1,0:T(4,128)(2,1)S(1)} %bitcast_convert_fusion.2, s32[4,2048]{1,0:T(4,128)S(1)} %get-tuple-element.109), kind=kOutput, calls=%fused_computation.5.clone.1 | convolution fusion | flops 542113792 | bytes 606208 | tf_op jit(solution)/shard_map/while/body/eval_jaxpr/csh,csl->chl/dot_general | solution.py:30
  42.5 3.8 %fusion.50 = f32[8,4,128,256]{3,2,1,0:T(8,128)} fusion(f32[8,4,128,256]{3,2,1,0:T(8,128)} %get-tuple-element.116, s32[]{:T(128)S(6)} %copy.30, f32[4,128,256]{2,1,0:T(8,128)S(1)} %fusion.48, s32[4,2048]{1,0:T(4,128)S(1)} %add_select_fusion.5, bf16[4,2048]{1,0:T(4,128)(2,1)S(1)} %fusion.49, s32[4,2048]{1,0:T(4,128)S(1)} %get-tuple-element.109), kind=kOutput, calls=%fused_computation.18.clone.1 | convolution fusion | flops 542244864 | bytes 1130500 | tf_op jit(solution)/shard_map/while/body/eval_jaxpr/csh,csl->chl/dot_general | solution.py:33
  46.4 0.1 add_select_fusion.4
  46.5 3.2 %fusion.48 = f32[4,128,256]{2,1,0:T(8,128)S(1)} fusion(s32[4,2048]{1,0:T(4,128)S(1)} %add_select_fusion.5, bf16[4,2048]{1,0:T(4,128)(2,1)S(1)} %bitcast_convert_fusion.2, s32[4,2048]{1,0:T(4,128)S(1)} %get-tuple-element.109), kind=kOutput, calls=%fused_computation.5.clone.1 | convolution fusion | flops 542113792 | bytes 606208 | tf_op jit(solution)/shard_map/while/body/eval_jaxpr/csh,csl->chl/dot_general | solution.py:30
  49.6 3.8 %fusion.50 = f32[8,4,128,256]{3,2,1,0:T(8,128)} fusion(f32[8,4,128,256]{3,2,1,0:T(8,128)} %get-tuple-element.116, s32[]{:T(128)S(6)} %copy.30, f32[4,128,256]{2,1,0:T(8,128)S(1)} %fusion.48, s32[4,2048]{1,0:T(4,128)S(1)} %add_select_fusion.5, bf16[4,2048]{1,0:T(4,128)(2,1)S(1)} %fusion.49, s32[4,2048]{1,0:T(4,128)S(1)} %get-tuple-element.109), kind=kOutput, calls=%fused_computation.18.clone.1 | convolution fusion | flops 542244864 | bytes 1130500 | tf_op jit(solution)/shard_map/while/body/eval_jaxpr/csh,csl->chl/dot_general | solution.py:33
  53.5 0.1 add_select_fusion.4
  53.6 3.2 %fusion.48 = f32[4,128,256]{2,1,0:T(8,128)S(1)} fusion(s32[4,2048]{1,0:T(4,128)S(1)} %add_select_fusion.5, bf16[4,2048]{1,0:T(4,128)(2,1)S(1)} %bitcast_convert_fusion.2, s32[4,2048]{1,0:T(4,128)S(1)} %get-tuple-element.109), kind=kOutput, calls=%fused_computation.5.clone.1 | convolution fusion | flops 542113792 | bytes 606208 | tf_op jit(solution)/shard_map/while/body/eval_jaxpr/csh,csl->chl/dot_general | solution.py:30
  56.7 3.8 %fusion.50 = f32[8,4,128,256]{3,2,1,0:T(8,128)} fusion(f32[8,4,128,256]{3,2,1,0:T(8,128)} %get-tuple-element.116, s32[]{:T(128)S(6)} %copy.30, f32[4,128,256]{2,1,0:T(8,128)S(1)} %fusion.48, s32[4,2048]{1,0:T(4,128)S(1)} %add_select_fusion.5, bf16[4,2048]{1,0:T(4,128)(2,1)S(1)} %fusion.49, s32[4,2048]{1,0:T(4,128)S(1)} %get-tuple-element.109), kind=kOutput, calls=%fused_computation.18.clone.1 | convolution fusion | flops 542244864 | bytes 1130500 | tf_op jit(solution)/shard_map/while/body/eval_jaxpr/csh,csl->chl/dot_general | solution.py:33
  60.6 0.1 add_select_fusion.4
  60.7 3.2 %fusion.48 = f32[4,128,256]{2,1,0:T(8,128)S(1)} fusion(s32[4,2048]{1,0:T(4,128)S(1)} %add_select_fusion.5, bf16[4,2048]{1,0:T(4,128)(2,1)S(1)} %bitcast_convert_fusion.2, s32[4,2048]{1,0:T(4,128)S(1)} %get-tuple-element.109), kind=kOutput, calls=%fused_computation.5.clone.1 | convolution fusion | flops 542113792 | bytes 606208 | tf_op jit(solution)/shard_map/while/body/eval_jaxpr/csh,csl->chl/dot_general | solution.py:30
  63.8 3.8 %fusion.50 = f32[8,4,128,256]{3,2,1,0:T(8,128)} fusion(f32[8,4,128,256]{3,2,1,0:T(8,128)} %get-tuple-element.116, s32[]{:T(128)S(6)} %copy.30, f32[4,128,256]{2,1,0:T(8,128)S(1)} %fusion.48, s32[4,2048]{1,0:T(4,128)S(1)} %add_select_fusion.5, bf16[4,2048]{1,0:T(4,128)(2,1)S(1)} %fusion.49, s32[4,2048]{1,0:T(4,128)S(1)} %get-tuple-element.109), kind=kOutput, calls=%fused_computation.18.clone.1 | convolution fusion | flops 542244864 | bytes 1130500 | tf_op jit(solution)/shard_map/while/body/eval_jaxpr/csh,csl->chl/dot_general | solution.py:33
  67.7 0.0 copy-start.1
  67.7 2.6 %fusion.39 = (f32[128,256]{1,0:T(8,128)S(1)}, f32[128,256]{1,0:T(8,128)S(1)}) fusion(f32[8,4,128,256]{3,2,1,0:T(8,128)} %get-tuple-element.58), kind=kLoop, calls=%fused_computation.62 | loop fusion | flops 3080192 | bytes 4456448 | tf_op jit(solution)/shard_map/reduce_sum | solution.py:61
  70.3 0.1 copy.24
  70.4 0.1 copy.25
  70.6 0.9 pad_maximum_fusion
  71.5 0.0 all-reduce.2.cloned.1.call-update
  71.6 0.0 copy-done.1
  71.6 4.4 %copy.26 = bf16[4,8,128,256]{3,1,2,0:T(8,128)(2,1)S(1)} copy(f32[4,8,128,256]{3,2,1,0:T(8,128)} %bitcast.62) | data formatting | bytes 6291456
  76.0 6.0 %copy.21 = bf16[32,32768]{0,1:T(8,128)(2,1)} copy(bf16[32,32768]{1,0:T(8,128)(2,1)S(1)} %bitcast.63) | data formatting | bytes 4194304 | tf_op jit(solution)/shard_map/reshape | solution.py:60
  82.0 10.1 %gather_fusion = bf16[2048,32]{1,0:T(8,128)(2,1)S(1)} fusion(bf16[32,32768]{0,1:T(8,128)(2,1)} %copy.21, s32[2048]{0:T(1024)S(1)} %fusion.38), kind=kCustom, calls=%fused_computation | custom fusion | bytes 270336 | tf_op jit(solution)/shard_map/jit(_take)/gather | solution.py:73
  92.1 0.2 copy.22
  92.3 0.7 select_convert_fusion
  93.0 4.3 %all-to-all-start = ((bf16[32,2,1024]{2,0,1:T(8,128)(2,1)}), bf16[32,2,1024]{2,0,1:T(8,128)(2,1)S(1)}, u32[]{:S(2)}, u32[]{:S(2)}) async-start(bf16[32,2,1024]{2,0,1:T(8,128)(2,1)} %select_convert_fusion), calls=%async_computation | async-start | bytes 262144 | tf_op jit(solution)/shard_map/all_to_all | solution.py:79
  97.3 103.7 %all-reduce.2.cloned.1.call-done = f32[2,32768]{1,0:T(2,128)} async-done(((f32[2,32768]{1,0:T(2,128)}), f32[2,32768]{1,0:T(2,128)}) %all-reduce.2.cloned.1.call-update) | async-done | bytes 262160 | tf_op jit(solution)/shard_map/psum | solution.py:65
  201.0 0.0 copy-start
  201.0 8.9 %copy.23 = f32[2,32768]{0,1:T(8,128)} copy(f32[2,32768]{1,0:T(2,128)} %all-reduce.2.cloned.1.call-done) | data formatting | bytes 524288 | tf_op jit(solution)/shard_map/psum | solution.py:65
  209.9 11.2 %gather_fusion.1 = f32[2048,2]{1,0:T(8,128)S(1)} fusion(f32[2,32768]{0,1:T(8,128)} %copy.23, s32[2048]{0:T(1024)S(1)} %fusion.38), kind=kCustom, calls=%fused_computation.1 | custom fusion | bytes 40960 | tf_op jit(solution)/shard_map/jit(_take)/gather | solution.py:67
  221.2 0.3 select_bitcast_fusion
  221.5 0.0 copy-done
  221.5 0.2 dynamic-slice_multiply_fusion.2
  221.7 0.8 pad_maximum_fusion.1
  222.5 0.3 fusion.40
  222.9 0.4 dynamic-slice_reduce_fusion
  223.2 0.0 all-to-all-done
  223.2 0.7 fusion.34
  (29 shorter events, 0.5 us)
Async XLA Ops:
  7.2 193.8 %all-reduce.2.cloned.1.call-start = ((), (), s32[]{:S(2)}) async-start(), calls=%async_computation.1 | async-start | bytes 524288 | tf_op jit(solution)/shard_map/psum | solution.py:65
  67.7 3.9 %copy-start.1 = (s32[2048]{0:T(1024)S(1)}, s32[2048]{0:T(1024)}, u32[]{:S(2)}) copy-start(s32[2048]{0:T(1024)} %param.9) | copy-start | bytes 24580
  93.0 130.2 %all-to-all-start = ((bf16[32,2,1024]{2,0,1:T(8,128)(2,1)}), bf16[32,2,1024]{2,0,1:T(8,128)(2,1)S(1)}, u32[]{:S(2)}, u32[]{:S(2)}) async-start(bf16[32,2,1024]{2,0,1:T(8,128)(2,1)} %select_convert_fusion), calls=%async_computation | async-start | bytes 262144 | tf_op jit(solution)/shard_map/all_to_all | solution.py:79
  201.0 20.5 %copy-start = (f32[2,32768]{1,0:T(2,128)S(1)}, f32[2,32768]{1,0:T(2,128)}, u32[]{:S(2)}) copy-start(f32[2,32768]{1,0:T(2,128)} %all-reduce.2.cloned.1.call-done) | copy-start | bytes 786436
Sparse Core Ops, SparseCore 0:
  71.7 129.2 all-reduce.1
where the time goes:
time: 231 us
  waiting for transfers between devices  104 us (45%)
  matrix products  55.7 us (24%)
  local copies, waits for them, and re-layouts  41.3 us (18%)
  between operations  14.2 us (6%)
  other arithmetic  11.3 us (5%)
  starting transfers between devices  4.31 us (2%)
    psum x1, waiting for transfers between devices, per_device(): sums = lax.psum(terms, ('gx', 'gy', 'gz'))  104 us
    dot_general x8, matrix products, cell_block(): jnp.einsum('csh,csl->chl', high_table, lower_table, preferred_element_typ...  30.5 us
    dot_general x8, matrix products, cell_block(): jnp.einsum('csh,csl->chl', high_table, upper_table, preferred_element_typ...  25.2 us
    gather x1, local copies, waits for them, and re-layouts, per_device(): picked_sums = jnp.take(sums, selected, axis=1)  11.2 us
    gather x2, local copies, waits for them, and re-layouts, per_device(): dense = jnp.take(expanded, selected, axis=1)  10.3 us
    psum x1, local copies, waits for them, and re-layouts, per_device(): sums = lax.psum(terms, ('gx', 'gy', 'gz'))  8.92 us
    reshape x1, local copies, waits for them, and re-layouts, per_device(): expanded = expanded.reshape(local_cells, GENES)  5.99 us
    unnamed x7, local copies, waits for them, and re-layouts  4.7 us
  transfers between devices with their start and end apart: 2, of which 1 were waited for; matrix products, arithmetic and copies ran while one was open for 19% of the time, Pallas kernels for 0%

commit v1 on v0

--- a/solution.py
+++ b/solution.py
@@ -62,7 +62,7 @@
     square = jnp.sum(expanded * expanded, axis=0)
     terms = jnp.stack([total, square])
     owned = GENES // owners
-    sums = lax.psum(terms, ("gx", "gy", "gz"))
+    sums = lax.psum(lax.psum(terms, ("gy", "gz")), "gx")
     own_sums = lax.dynamic_slice_in_dim(sums, owner_index * owned, owned, 1)
     picked_sums = jnp.take(sums, selected, axis=1)
     own_mean = own_sums[0] / cells

time: 231 us -> 210 us (0.909)
  waiting for transfers between devices: 104 us -> 82.9 us
    psum x1 -> x2, waiting for transfers between devices: 104 us -> 82.9 us  [per_device(): sums = lax.psum(lax.psum(terms, ('gy', 'gz')), 'gx')]
  transfers between devices with their start and end apart: 2 -> 3, of which waited for: 1 -> 2; matrix products, arithmetic and copies ran while one was open for 19% -> 21% of each run, Pallas kernels for 0% -> 0%
where the time goes in v1:
time: 210 us; the launch traced here: 209 us
  waiting for transfers between devices  82.9 us (39%)
  matrix products  55.7 us (27%)
  local copies, waits for them, and re-layouts  41.3 us (20%)
  between operations  14.2 us (7%)
  other arithmetic  11.2 us (5%)
  starting transfers between devices  3.46 us (2%)
    psum x2, waiting for transfers between devices, per_device(): sums = lax.psum(lax.psum(terms, ('gy', 'gz')), 'gx')  82.9 us
    dot_general x8, matrix products, cell_block(): jnp.einsum('csh,csl->chl', high_table, lower_table, preferred_element_typ...  30.5 us
    dot_general x8, matrix products, cell_block(): jnp.einsum('csh,csl->chl', high_table, upper_table, preferred_element_typ...  25.2 us
    gather x1, local copies, waits for them, and re-layouts, per_device(): picked_sums = jnp.take(sums, selected, axis=1)  11.2 us
    gather x2, local copies, waits for them, and re-layouts, per_device(): dense = jnp.take(expanded, selected, axis=1)  10.3 us
    psum x1, local copies, waits for them, and re-layouts, per_device(): sums = lax.psum(lax.psum(terms, ('gy', 'gz')), 'gx')  8.92 us
    reshape x1, local copies, waits for them, and re-layouts, per_device(): expanded = expanded.reshape(local_cells, GENES)  5.99 us
    unnamed x7, local copies, waits for them, and re-layouts  4.7 us
  transfers between devices with their start and end apart: 3, of which 2 were waited for; matrix products, arithmetic and copies ran while one was open for 21% of the time, Pallas kernels for 0%

profile of v1, /device:TPU:0, one launch (start us, length us, event | category | flops | bytes accessed | tf_op | source)
XLA Modules:
  0.0 209.1 jit_solution(2722997652265311202)
XLA Ops:
  7.2 0.0 all-reduce.3.cloned.1.call-start
  7.2 1.2 fusion.36
  8.4 1.1 multiply_log-plus-one_fusion
  9.5 0.1 reshape.103
  9.6 1.0 fusion.35
  10.7 0.1 reshape.102
  10.8 56.9 %while.12 = (s32[]{:T(128)}, f32[8,4,128,256]{3,2,1,0:T(8,128)}, s32[8,4,2048]{2,1,0:T(4,128)S(1)}, f32[8,4,2048]{2,1,0:T(4,128)S(1)}, s32[]{:T(128)}) while((s32[]{:T(128)}, f32[8,4,128,256]{3,2,1,0:T(8,128)}, s32[8,4,2048]{2,1,0:T(4,128)S(1)}, f32[8,4,2048]{2,1,0:T(4,128)S(1)}, s32[]{:T(128)}) %tuple.39), condition=%wide.region_2.3_spmd, body=%wide.region_1.2_spmd.sunk | while | flops 1084588032 | bytes 1982553 | solution.py:53
  10.8 0.1 add_select_fusion.4
  10.9 3.2 %fusion.48 = f32[4,128,256]{2,1,0:T(8,128)S(1)} fusion(s32[4,2048]{1,0:T(4,128)S(1)} %add_select_fusion.5, bf16[4,2048]{1,0:T(4,128)(2,1)S(1)} %bitcast_convert_fusion.2, s32[4,2048]{1,0:T(4,128)S(1)} %get-tuple-element.109), kind=kOutput, calls=%fused_computation.5.clone.1 | convolution fusion | flops 542113792 | bytes 606208 | tf_op jit(solution)/shard_map/while/body/eval_jaxpr/csh,csl->chl/dot_general | solution.py:30
  14.1 3.8 %fusion.50 = f32[8,4,128,256]{3,2,1,0:T(8,128)} fusion(f32[8,4,128,256]{3,2,1,0:T(8,128)} %get-tuple-element.116, s32[]{:T(128)S(6)} %copy.30, f32[4,128,256]{2,1,0:T(8,128)S(1)} %fusion.48, s32[4,2048]{1,0:T(4,128)S(1)} %add_select_fusion.5, bf16[4,2048]{1,0:T(4,128)(2,1)S(1)} %fusion.49, s32[4,2048]{1,0:T(4,128)S(1)} %get-tuple-element.109), kind=kOutput, calls=%fused_computation.18.clone.1 | convolution fusion | flops 542244864 | bytes 1130500 | tf_op jit(solution)/shard_map/while/body/eval_jaxpr/csh,csl->chl/dot_general | solution.py:33
  17.9 0.1 add_select_fusion.4
  18.0 3.2 %fusion.48 = f32[4,128,256]{2,1,0:T(8,128)S(1)} fusion(s32[4,2048]{1,0:T(4,128)S(1)} %add_select_fusion.5, bf16[4,2048]{1,0:T(4,128)(2,1)S(1)} %bitcast_convert_fusion.2, s32[4,2048]{1,0:T(4,128)S(1)} %get-tuple-element.109), kind=kOutput, calls=%fused_computation.5.clone.1 | convolution fusion | flops 542113792 | bytes 606208 | tf_op jit(solution)/shard_map/while/body/eval_jaxpr/csh,csl->chl/dot_general | solution.py:30
  21.2 3.8 %fusion.50 = f32[8,4,128,256]{3,2,1,0:T(8,128)} fusion(f32[8,4,128,256]{3,2,1,0:T(8,128)} %get-tuple-element.116, s32[]{:T(128)S(6)} %copy.30, f32[4,128,256]{2,1,0:T(8,128)S(1)} %fusion.48, s32[4,2048]{1,0:T(4,128)S(1)} %add_select_fusion.5, bf16[4,2048]{1,0:T(4,128)(2,1)S(1)} %fusion.49, s32[4,2048]{1,0:T(4,128)S(1)} %get-tuple-element.109), kind=kOutput, calls=%fused_computation.18.clone.1 | convolution fusion | flops 542244864 | bytes 1130500 | tf_op jit(solution)/shard_map/while/body/eval_jaxpr/csh,csl->chl/dot_general | solution.py:33
  25.0 0.1 add_select_fusion.4
  25.1 3.2 %fusion.48 = f32[4,128,256]{2,1,0:T(8,128)S(1)} fusion(s32[4,2048]{1,0:T(4,128)S(1)} %add_select_fusion.5, bf16[4,2048]{1,0:T(4,128)(2,1)S(1)} %bitcast_convert_fusion.2, s32[4,2048]{1,0:T(4,128)S(1)} %get-tuple-element.109), kind=kOutput, calls=%fused_computation.5.clone.1 | convolution fusion | flops 542113792 | bytes 606208 | tf_op jit(solution)/shard_map/while/body/eval_jaxpr/csh,csl->chl/dot_general | solution.py:30
  28.3 3.8 %fusion.50 = f32[8,4,128,256]{3,2,1,0:T(8,128)} fusion(f32[8,4,128,256]{3,2,1,0:T(8,128)} %get-tuple-element.116, s32[]{:T(128)S(6)} %copy.30, f32[4,128,256]{2,1,0:T(8,128)S(1)} %fusion.48, s32[4,2048]{1,0:T(4,128)S(1)} %add_select_fusion.5, bf16[4,2048]{1,0:T(4,128)(2,1)S(1)} %fusion.49, s32[4,2048]{1,0:T(4,128)S(1)} %get-tuple-element.109), kind=kOutput, calls=%fused_computation.18.clone.1 | convolution fusion | flops 542244864 | bytes 1130500 | tf_op jit(solution)/shard_map/while/body/eval_jaxpr/csh,csl->chl/dot_general | solution.py:33
  32.1 0.1 add_select_fusion.4
  32.3 3.2 %fusion.48 = f32[4,128,256]{2,1,0:T(8,128)S(1)} fusion(s32[4,2048]{1,0:T(4,128)S(1)} %add_select_fusion.5, bf16[4,2048]{1,0:T(4,128)(2,1)S(1)} %bitcast_convert_fusion.2, s32[4,2048]{1,0:T(4,128)S(1)} %get-tuple-element.109), kind=kOutput, calls=%fused_computation.5.clone.1 | convolution fusion | flops 542113792 | bytes 606208 | tf_op jit(solution)/shard_map/while/body/eval_jaxpr/csh,csl->chl/dot_general | solution.py:30
  35.4 3.8 %fusion.50 = f32[8,4,128,256]{3,2,1,0:T(8,128)} fusion(f32[8,4,128,256]{3,2,1,0:T(8,128)} %get-tuple-element.116, s32[]{:T(128)S(6)} %copy.30, f32[4,128,256]{2,1,0:T(8,128)S(1)} %fusion.48, s32[4,2048]{1,0:T(4,128)S(1)} %add_select_fusion.5, bf16[4,2048]{1,0:T(4,128)(2,1)S(1)} %fusion.49, s32[4,2048]{1,0:T(4,128)S(1)} %get-tuple-element.109), kind=kOutput, calls=%fused_computation.18.clone.1 | convolution fusion | flops 542244864 | bytes 1130500 | tf_op jit(solution)/shard_map/while/body/eval_jaxpr/csh,csl->chl/dot_general | solution.py:33
  39.3 0.1 add_select_fusion.4
  39.4 3.2 %fusion.48 = f32[4,128,256]{2,1,0:T(8,128)S(1)} fusion(s32[4,2048]{1,0:T(4,128)S(1)} %add_select_fusion.5, bf16[4,2048]{1,0:T(4,128)(2,1)S(1)} %bitcast_convert_fusion.2, s32[4,2048]{1,0:T(4,128)S(1)} %get-tuple-element.109), kind=kOutput, calls=%fused_computation.5.clone.1 | convolution fusion | flops 542113792 | bytes 606208 | tf_op jit(solution)/shard_map/while/body/eval_jaxpr/csh,csl->chl/dot_general | solution.py:30
  42.5 3.8 %fusion.50 = f32[8,4,128,256]{3,2,1,0:T(8,128)} fusion(f32[8,4,128,256]{3,2,1,0:T(8,128)} %get-tuple-element.116, s32[]{:T(128)S(6)} %copy.30, f32[4,128,256]{2,1,0:T(8,128)S(1)} %fusion.48, s32[4,2048]{1,0:T(4,128)S(1)} %add_select_fusion.5, bf16[4,2048]{1,0:T(4,128)(2,1)S(1)} %fusion.49, s32[4,2048]{1,0:T(4,128)S(1)} %get-tuple-element.109), kind=kOutput, calls=%fused_computation.18.clone.1 | convolution fusion | flops 542244864 | bytes 1130500 | tf_op jit(solution)/shard_map/while/body/eval_jaxpr/csh,csl->chl/dot_general | solution.py:33
  46.4 0.1 add_select_fusion.4
  46.5 3.2 %fusion.48 = f32[4,128,256]{2,1,0:T(8,128)S(1)} fusion(s32[4,2048]{1,0:T(4,128)S(1)} %add_select_fusion.5, bf16[4,2048]{1,0:T(4,128)(2,1)S(1)} %bitcast_convert_fusion.2, s32[4,2048]{1,0:T(4,128)S(1)} %get-tuple-element.109), kind=kOutput, calls=%fused_computation.5.clone.1 | convolution fusion | flops 542113792 | bytes 606208 | tf_op jit(solution)/shard_map/while/body/eval_jaxpr/csh,csl->chl/dot_general | solution.py:30
  49.6 3.8 %fusion.50 = f32[8,4,128,256]{3,2,1,0:T(8,128)} fusion(f32[8,4,128,256]{3,2,1,0:T(8,128)} %get-tuple-element.116, s32[]{:T(128)S(6)} %copy.30, f32[4,128,256]{2,1,0:T(8,128)S(1)} %fusion.48, s32[4,2048]{1,0:T(4,128)S(1)} %add_select_fusion.5, bf16[4,2048]{1,0:T(4,128)(2,1)S(1)} %fusion.49, s32[4,2048]{1,0:T(4,128)S(1)} %get-tuple-element.109), kind=kOutput, calls=%fused_computation.18.clone.1 | convolution fusion | flops 542244864 | bytes 1130500 | tf_op jit(solution)/shard_map/while/body/eval_jaxpr/csh,csl->chl/dot_general | solution.py:33
  53.5 0.1 add_select_fusion.4
  53.6 3.2 %fusion.48 = f32[4,128,256]{2,1,0:T(8,128)S(1)} fusion(s32[4,2048]{1,0:T(4,128)S(1)} %add_select_fusion.5, bf16[4,2048]{1,0:T(4,128)(2,1)S(1)} %bitcast_convert_fusion.2, s32[4,2048]{1,0:T(4,128)S(1)} %get-tuple-element.109), kind=kOutput, calls=%fused_computation.5.clone.1 | convolution fusion | flops 542113792 | bytes 606208 | tf_op jit(solution)/shard_map/while/body/eval_jaxpr/csh,csl->chl/dot_general | solution.py:30
  56.7 3.8 %fusion.50 = f32[8,4,128,256]{3,2,1,0:T(8,128)} fusion(f32[8,4,128,256]{3,2,1,0:T(8,128)} %get-tuple-element.116, s32[]{:T(128)S(6)} %copy.30, f32[4,128,256]{2,1,0:T(8,128)S(1)} %fusion.48, s32[4,2048]{1,0:T(4,128)S(1)} %add_select_fusion.5, bf16[4,2048]{1,0:T(4,128)(2,1)S(1)} %fusion.49, s32[4,2048]{1,0:T(4,128)S(1)} %get-tuple-element.109), kind=kOutput, calls=%fused_computation.18.clone.1 | convolution fusion | flops 542244864 | bytes 1130500 | tf_op jit(solution)/shard_map/while/body/eval_jaxpr/csh,csl->chl/dot_general | solution.py:33
  60.6 0.1 add_select_fusion.4
  60.7 3.2 %fusion.48 = f32[4,128,256]{2,1,0:T(8,128)S(1)} fusion(s32[4,2048]{1,0:T(4,128)S(1)} %add_select_fusion.5, bf16[4,2048]{1,0:T(4,128)(2,1)S(1)} %bitcast_convert_fusion.2, s32[4,2048]{1,0:T(4,128)S(1)} %get-tuple-element.109), kind=kOutput, calls=%fused_computation.5.clone.1 | convolution fusion | flops 542113792 | bytes 606208 | tf_op jit(solution)/shard_map/while/body/eval_jaxpr/csh,csl->chl/dot_general | solution.py:30
  63.8 3.8 %fusion.50 = f32[8,4,128,256]{3,2,1,0:T(8,128)} fusion(f32[8,4,128,256]{3,2,1,0:T(8,128)} %get-tuple-element.116, s32[]{:T(128)S(6)} %copy.30, f32[4,128,256]{2,1,0:T(8,128)S(1)} %fusion.48, s32[4,2048]{1,0:T(4,128)S(1)} %add_select_fusion.5, bf16[4,2048]{1,0:T(4,128)(2,1)S(1)} %fusion.49, s32[4,2048]{1,0:T(4,128)S(1)} %get-tuple-element.109), kind=kOutput, calls=%fused_computation.18.clone.1 | convolution fusion | flops 542244864 | bytes 1130500 | tf_op jit(solution)/shard_map/while/body/eval_jaxpr/csh,csl->chl/dot_general | solution.py:33
  67.7 0.0 copy-start.1
  67.7 2.6 %fusion.39 = (f32[128,256]{1,0:T(8,128)S(1)}, f32[128,256]{1,0:T(8,128)S(1)}) fusion(f32[8,4,128,256]{3,2,1,0:T(8,128)} %get-tuple-element.58), kind=kLoop, calls=%fused_computation.62 | loop fusion | flops 3080192 | bytes 4456448 | tf_op jit(solution)/shard_map/reduce_sum | solution.py:61
  70.3 0.1 copy.24
  70.4 0.1 copy.25
  70.6 0.9 pad_maximum_fusion
  71.5 0.0 all-reduce.3.cloned.1.call-update
  71.6 0.0 all-reduce.5.cloned.1.call-start
  71.6 0.0 copy-done.1
  71.6 4.4 %copy.26 = bf16[4,8,128,256]{3,1,2,0:T(8,128)(2,1)S(1)} copy(f32[4,8,128,256]{3,2,1,0:T(8,128)} %bitcast.62) | data formatting | bytes 6291456
  76.1 6.0 %copy.21 = bf16[32,32768]{0,1:T(8,128)(2,1)} copy(bf16[32,32768]{1,0:T(8,128)(2,1)S(1)} %bitcast.63) | data formatting | bytes 4194304 | tf_op jit(solution)/shard_map/reshape | solution.py:60
  82.1 10.1 %gather_fusion = bf16[2048,32]{1,0:T(8,128)(2,1)S(1)} fusion(bf16[32,32768]{0,1:T(8,128)(2,1)} %copy.21, s32[2048]{0:T(1024)S(1)} %fusion.38), kind=kCustom, calls=%fused_computation | custom fusion | bytes 270336 | tf_op jit(solution)/shard_map/jit(_take)/gather | solution.py:73
  92.1 0.2 copy.22
  92.3 53.1 %all-reduce.3.cloned.1.call-done = f32[2,32768]{1,0:T(2,128)} async-done(((f32[2,32768]{1,0:T(2,128)}), f32[2,32768]{1,0:T(2,128)}) %all-reduce.3.cloned.1.call-update) | async-done | bytes 262160 | tf_op jit(solution)/shard_map/psum | solution.py:65
  145.5 0.0 all-reduce.5.cloned.1.call-update
  145.5 0.7 select_convert_fusion
  146.2 3.4 %all-to-all-start = ((bf16[32,2,1024]{2,0,1:T(8,128)(2,1)}), bf16[32,2,1024]{2,0,1:T(8,128)(2,1)S(1)}, u32[]{:S(2)}, u32[]{:S(2)}) async-start(bf16[32,2,1024]{2,0,1:T(8,128)(2,1)} %select_convert_fusion), calls=%async_computation | async-start | bytes 262144 | tf_op jit(solution)/shard_map/all_to_all | solution.py:79
  149.6 29.7 %all-reduce.5.cloned.1.call-done = f32[2,32768]{1,0:T(2,128)} async-done(((f32[2,32768]{1,0:T(2,128)}), f32[2,32768]{1,0:T(2,128)}) %all-reduce.5.cloned.1.call-update) | async-done | bytes 262160 | tf_op jit(solution)/shard_map/psum | solution.py:65
  179.3 0.0 copy-start
  179.3 8.9 %copy.23 = f32[2,32768]{0,1:T(8,128)} copy(f32[2,32768]{1,0:T(2,128)} %all-reduce.5.cloned.1.call-done) | data formatting | bytes 524288 | tf_op jit(solution)/shard_map/psum | solution.py:65
  188.2 11.2 %gather_fusion.1 = f32[2048,2]{1,0:T(8,128)S(1)} fusion(f32[2,32768]{0,1:T(8,128)} %copy.23, s32[2048]{0:T(1024)S(1)} %fusion.38), kind=kCustom, calls=%fused_computation.1 | custom fusion | bytes 40960 | tf_op jit(solution)/shard_map/jit(_take)/gather | solution.py:67
  199.5 0.3 select_bitcast_fusion
  199.8 0.0 copy-done
  199.8 0.2 dynamic-slice_multiply_fusion.2
  200.0 0.8 pad_maximum_fusion.1
  200.8 0.3 fusion.40
  201.2 0.4 dynamic-slice_reduce_fusion
  201.5 0.0 all-to-all-done
  201.5 0.7 fusion.34
  (29 shorter events, 0.5 us)
Async XLA Ops:
  7.2 138.3 %all-reduce.3.cloned.1.call-start = ((), (), s32[]{:S(2)}) async-start(), calls=%async_computation.1 | async-start | bytes 524288 | tf_op jit(solution)/shard_map/psum | solution.py:65
  67.7 4.0 %copy-start.1 = (s32[2048]{0:T(1024)S(1)}, s32[2048]{0:T(1024)}, u32[]{:S(2)}) copy-start(s32[2048]{0:T(1024)} %param.9) | copy-start | bytes 24580
  71.6 107.7 %all-reduce.5.cloned.1.call-start = ((), (), s32[]{:S(2)}) async-start(), calls=%async_computation.2 | async-start | bytes 524288 | tf_op jit(solution)/shard_map/psum | solution.py:65
  146.2 55.4 %all-to-all-start = ((bf16[32,2,1024]{2,0,1:T(8,128)(2,1)}), bf16[32,2,1024]{2,0,1:T(8,128)(2,1)S(1)}, u32[]{:S(2)}, u32[]{:S(2)}) async-start(bf16[32,2,1024]{2,0,1:T(8,128)(2,1)} %select_convert_fusion), calls=%async_computation | async-start | bytes 262144 | tf_op jit(solution)/shard_map/all_to_all | solution.py:79
  179.3 20.5 %copy-start = (f32[2,32768]{1,0:T(2,128)S(1)}, f32[2,32768]{1,0:T(2,128)}, u32[]{:S(2)}) copy-start(f32[2,32768]{1,0:T(2,128)} %all-reduce.5.cloned.1.call-done) | copy-start | bytes 786436
Sparse Core Ops, SparseCore 0:
  71.7 73.7 all-reduce.2
  147.8 31.4 all-reduce.4
